TPU v7x, 32 devices: a whole 2x2x4 slice. The times are simulated.
32 devices in a mesh: kpt: 2 (over y), row: 4 (over x, core), col: 4 (over z).
Axes of the slice: x: 2, y: 2, z: 4, core: 2. Of those that a mesh axis runs over, the one named last changes fastest.
Arguments:
- left_blocks: bfloat16 [8, 64, 2, 2, 128, 128], P(('kpt', 'row'), 'col'), parts along dimension 0, may hold values from -0.5 to 0.5
- left_rows: int32 [8, 64, 2], P(('kpt', 'row'), 'col'), parts along dimension 0, may hold values from 0 to 7, as said below
- left_count: int32 [8, 64], P(('kpt', 'row'), 'col'), parts along dimension 0, may hold values from 1 to 2, as said below
- left_level: int32 [8, 64, 2], P(('kpt', 'row'), 'col'), parts along dimension 0, may hold values from 0 to 7
- right_blocks: bfloat16 [2, 64, 4, 4, 2, 128, 128], P('kpt', 'row', 'col'), parts along dimension 0, may hold values from -6 to 6
- right_cols: int32 [2, 64, 4, 4], P('kpt', 'row', 'col'), parts along dimension 0, may hold values from 0 to 15, as said below
- right_count: int32 [2, 64, 4], P('kpt', 'row', 'col'), parts along dimension 0, may hold values from 1 to 4, as said below
- right_level: int32 [2, 64, 4, 4], P('kpt', 'row', 'col'), parts along dimension 0, may hold values from 0 to 7
Outputs:
- product_blocks: bfloat16 [64, 64, 2, 128, 128], P(('kpt', 'row'), 'col'), parts along dimension 0
There are 2 independent parts, one for each index of `kpt`. A program takes and returns all parts, laid end to end along the dimension named above; each array names one. Nothing has to cross between parts.
Inputs may be any that keep to these rules, and one draw needn't show every extreme that they name: `left_rows`: the 2 slots of one row group and block column name distinct block rows. `left_count`: in every row group some block column has all 2 slots live. `right_cols`: the 4 slots of one block row and column group name distinct block columns. `right_count`: in every column group some block row has all 4 slots live.
All inputs are finite; a program needn't handle non-finite values.
Results may differ from a plain program's by a relative error of at most 0.001.
Values may be sent and summed in bfloat16 or wider, within the bound.
A program may use at most 256 MiB of HBM per device.

v0:
```python
import jax
import jax.numpy as jnp
from jax import lax
from jax.sharding import PartitionSpec as P

GR = 8
LEVEL_CUT = 7


def pair_products(left_pack, right_pack, total):
    left_blocks, left_rows, left_count, left_level = left_pack
    right_blocks, right_cols, right_count, right_level = right_pack
    slots_left = left_rows.shape[1]
    slots_right = right_cols.shape[1]
    live_left = jnp.arange(slots_left, dtype=jnp.int32)[None, :] < left_count[:, None]
    live_right = jnp.arange(slots_right, dtype=jnp.int32)[None, :] < right_count[:, None]
    kept = live_left[:, :, None] & live_right[:, None, :]
    kept = kept & (left_level[:, :, None] + right_level[:, None, :] >= LEVEL_CUT)
    terms = jnp.einsum(
        "kmcij,kndjl->kmncdil", left_blocks, right_blocks, preferred_element_type=jnp.float32
    )
    real_part = terms[:, :, :, 0, 0] - terms[:, :, :, 1, 1]
    imag_part = terms[:, :, :, 0, 1] + terms[:, :, :, 1, 0]
    product = jnp.stack([real_part, imag_part], axis=3) * kept[:, :, :, None, None, None].astype(
        jnp.float32
    )
    row_index = jnp.broadcast_to(left_rows[:, :, None], kept.shape).reshape(-1)
    col_index = jnp.broadcast_to(right_cols[:, None, :], kept.shape).reshape(-1)
    width = left_blocks.shape[-1]
    return total.at[row_index, col_index].add(product.reshape(-1, 2, width, width))


def body(
    left_blocks,
    left_rows,
    left_count,
    left_level,
    right_blocks,
    right_cols,
    right_count,
    right_level,
):
    left_pack = (left_blocks[0], left_rows[0], left_count[0], left_level[0])
    right_pack = (
        right_blocks[:, :, 0],
        right_cols[:, :, 0],
        right_count[:, :, 0],
        right_level[:, :, 0],
    )
    width = left_blocks.shape[-1]
    panel_rows = left_blocks.shape[1]
    total = jnp.zeros((GR, panel_rows, 2, width, width), jnp.float32)
    whole = (
        lax.all_gather(right_pack[0], "row", axis=1, tiled=True),
        lax.all_gather(right_pack[1], "row", axis=1, tiled=True),
        lax.all_gather(right_pack[2], "row", axis=1, tiled=True),
        lax.all_gather(right_pack[3], "row", axis=1, tiled=True),
    )
    merged = whole[0].shape[0] * whole[0].shape[1]
    flat = jax.tree.map(lambda member: member.reshape((merged,) + member.shape[2:]), whole)
    carry = total
    piece = (
        lax.all_gather(left_pack[0], "col", axis=0, tiled=True),
        lax.all_gather(left_pack[1], "col", axis=0, tiled=True),
        lax.all_gather(left_pack[2], "col", axis=0, tiled=True),
        lax.all_gather(left_pack[3], "col", axis=0, tiled=True),
    )
    count = piece[0].shape[0]
    for first in range(0, count, panel_rows):
        size = min(panel_rows, count - first)
        left_part = jax.tree.map(lambda member: member[first : first + size], piece)
        right_part = jax.tree.map(
            lambda member: lax.dynamic_slice_in_dim(member, first, size, 0), flat
        )
        carry = pair_products(left_part, right_part, carry)
    total = carry
    return total.astype(jnp.bfloat16)


def solution(mesh):
    in_specs = (
        P(("kpt", "row"), "col", None, None, None, None),
        P(("kpt", "row"), "col", None),
        P(("kpt", "row"), "col"),
        P(("kpt", "row"), "col", None),
        P("kpt", "row", "col", None, None, None, None),
        P("kpt", "row", "col", None),
        P("kpt", "row", "col"),
        P("kpt", "row", "col", None),
    )
    out_specs = P(("kpt", "row"), "col", None, None, None)
    return jax.shard_map(body, mesh=mesh, in_specs=in_specs, out_specs=out_specs, check_vma=False)
```

profile of v0, /device:TPU:1, one launch (start us, length us, event | category | flops | bytes accessed | tf_op | source)
XLA Modules:
  0.0 728.5 jit_solution(17531730856529968428)
XLA Ops:
  6.5 0.7 all-gather.11.cloned.1.call-update
  8.0 1.2 dynamic-slice.1
  9.3 1.2 dynamic-slice
  11.7 0.8 copy.67
  12.4 0.8 copy.70
  13.2 11.6 %all-gather.6 = s32[1,64,2]{2,0,1:T(1,128)S(1)} all-gather(s32[1,16,2]{2,0,1:T(1,128)S(1)} %copy.67), channel_id=8, replica_groups=mesh['kpt'=2,'row'=4,'col'=4] {'col'}, dimensions={1}, use_global_device_ids=true | all-gather | bytes 640 | tf_op jit(solution)/shard_map/all_gather | solution.py:66
  24.8 0.7 bitcast_dynamic-update-slice_fusion
  25.5 7.5 %all-reduce.1 = s32[64]{0:T(128)S(1)} all-reduce(s32[64]{0:T(128)S(1)} %bitcast_dynamic-update-slice_fusion), channel_id=7, replica_groups=mesh['kpt'=2,'row'=4,'col'=4] {'row'}, use_global_device_ids=true, to_apply=%add.1 | all-reduce | flops 64 | bytes 512
  33.0 0.7 bitcast_dynamic-update-slice_fusion.1
  33.7 6.5 all-reduce
  40.2 7.5 %all-gather.7 = s32[1,64,1,4]{3,2,0,1:T(1,128)S(1)} all-gather(s32[1,16,1,4]{3,2,0,1:T(1,128)S(1)} %copy.70), channel_id=9, replica_groups=mesh['kpt'=2,'row'=4,'col'=4] {'row'}, dimensions={1}, use_global_device_ids=true | all-gather | bytes 1280 | tf_op jit(solution)/shard_map/all_gather | solution.py:57
  48.3 0.8 copy.55
  49.0 10.2 %all-gather = s32[1,64,2]{2,0,1:T(1,128)S(1)} all-gather(s32[1,16,2]{2,0,1:T(1,128)S(1)} %copy.55), channel_id=2, replica_groups=mesh['kpt'=2,'row'=4,'col'=4] {'col'}, dimensions={1}, use_global_device_ids=true | all-gather | bytes 640 | tf_op jit(solution)/shard_map/all_gather | solution.py:64
  59.5 0.8 copy.58
  60.2 8.3 %all-gather.1 = s32[1,64,1,4]{3,2,0,1:T(1,128)S(1)} all-gather(s32[1,16,1,4]{3,2,0,1:T(1,128)S(1)} %copy.58), channel_id=3, replica_groups=mesh['kpt'=2,'row'=4,'col'=4] {'row'}, dimensions={1}, use_global_device_ids=true | all-gather | bytes 1280 | tf_op jit(solution)/shard_map/all_gather | solution.py:55
  73.9 43.8 %all-gather.11.cloned.1.call-done = bf16[1,64,1,4,2,128,128]{6,5,4,3,2,0,1:T(8,128)(2,1)} async-done(((bf16[1,16,1,4,2,128,128]{6,5,4,3,2,0,1:T(8,128)(2,1)}), bf16[1,64,1,4,2,128,128]{6,5,4,3,2,0,1:T(8,128)(2,1)}) %all-gather.11.cloned.1.call-update) | async-done | bytes 16777232 | tf_op jit(solution)/shard_map/all_gather | solution.py:54
  117.7 22.7 %copy.62 = bf16[1,64,1,4,2,128,128]{5,6,4,3,1,2,0:T(8,128)(2,1)} copy(bf16[1,64,1,4,2,128,128]{6,5,4,3,2,0,1:T(8,128)(2,1)} %all-gather.11.cloned.1.call-done) | data formatting | bytes 33554432 | tf_op jit(solution)/shard_map/all_gather | solution.py:54
  140.5 128.2 %all-gather.13.cloned.1.call-done = bf16[1,64,2,2,128,128]{5,4,3,2,0,1:T(8,128)(2,1)} async-done(((bf16[1,16,2,2,128,128]{5,4,3,2,0,1:T(8,128)(2,1)}), bf16[1,64,2,2,128,128]{5,4,3,2,0,1:T(8,128)(2,1)}) %all-gather.13.cloned.1.call-update) | async-done | bytes 8388624 | tf_op jit(solution)/shard_map/all_gather | solution.py:63
  268.7 18.5 %convolution_bitcast_fusion.3 = f32[16,2,4,2,2,128,128]{5,6,3,1,4,2,0:T(8,128)} fusion(bf16[1,64,4,2,128,128]{4,5,3,2,1,0:T(8,128)(2,1)} %bitcast.137, bf16[1,64,2,2,128,128]{5,4,3,2,1,0:T(8,128)(2,1)} %bitcast.149), kind=kOutput, calls=%fused_computation.11 | convolution fusion | flops 2147483648 | bytes 39845888 | tf_op jit(solution)/shard_map/kmcij,kndjl->kmncdil/dot_general | solution.py:19
  287.2 18.5 %convolution_bitcast_fusion.2 = f32[16,2,4,2,2,128,128]{5,6,3,1,4,2,0:T(8,128)} fusion(bf16[1,64,4,2,128,128]{4,5,3,2,1,0:T(8,128)(2,1)} %bitcast.138, bf16[1,64,2,2,128,128]{5,4,3,2,1,0:T(8,128)(2,1)} %bitcast.150), kind=kOutput, calls=%fused_computation.10 | convolution fusion | flops 2147483648 | bytes 39845888 | tf_op jit(solution)/shard_map/kmcij,kndjl->kmncdil/dot_general | solution.py:19
  305.6 18.7 %convolution_bitcast_fusion.1 = f32[16,2,4,2,2,128,128]{5,6,3,1,4,2,0:T(8,128)} fusion(bf16[1,64,4,2,128,128]{4,5,3,2,1,0:T(8,128)(2,1)} %bitcast.139, bf16[1,64,2,2,128,128]{5,4,3,2,1,0:T(8,128)(2,1)} %bitcast.151), kind=kOutput, calls=%fused_computation.9 | convolution fusion | flops 2147483648 | bytes 39845888 | tf_op jit(solution)/shard_map/kmcij,kndjl->kmncdil/dot_general | solution.py:19
  324.3 18.5 %convolution_bitcast_fusion = f32[16,2,4,2,2,128,128]{5,6,3,1,4,2,0:T(8,128)} fusion(bf16[1,64,4,2,128,128]{4,5,3,2,1,0:T(8,128)(2,1)} %bitcast.140, bf16[1,64,2,2,128,128]{5,4,3,2,1,0:T(8,128)(2,1)} %bitcast.152), kind=kOutput, calls=%fused_computation.8 | convolution fusion | flops 2147483648 | bytes 39845888 | tf_op jit(solution)/shard_map/kmcij,kndjl->kmncdil/dot_general | solution.py:19
  342.7 19.3 %slice_subtract_fusion.3 = (f32[16,2,4,1,1,128,128]{5,6,3,1,4,2,0:T(8,128)}, f32[16,2,4,1,1,128,128]{5,6,3,1,4,2,0:T(8,128)}) fusion(f32[16,2,4,2,2,128,128]{5,6,3,1,4,2,0:T(8,128)} %convolution_bitcast_fusion.3), kind=kLoop, calls=%fused_computation.19 | loop fusion | flops 4194304 | bytes 50331648 | tf_op jit(solution)/shard_map/sub | solution.py:22
  362.1 9.3 %copy.65 = f32[16,2,4,1,1,128,128]{6,5,2,1,0,4,3:T(8,128)} copy(f32[16,2,4,1,1,128,128]{5,6,3,1,4,2,0:T(8,128)} %get-tuple-element.11) | data formatting | bytes 16777216 | tf_op jit(solution)/shard_map/sub | solution.py:22
  371.4 9.2 %copy.66 = f32[16,2,4,1,1,128,128]{6,5,2,1,0,4,3:T(8,128)} copy(f32[16,2,4,1,1,128,128]{5,6,3,1,4,2,0:T(8,128)} %get-tuple-element.12) | data formatting | bytes 16777216 | tf_op jit(solution)/shard_map/add | solution.py:23
  380.6 6.8 maximum_multiply_fusion
  387.4 6.0 copy.73
  393.4 19.4 %slice_subtract_fusion.2 = (f32[16,2,4,1,1,128,128]{5,6,3,1,4,2,0:T(8,128)}, f32[16,2,4,1,1,128,128]{5,6,3,1,4,2,0:T(8,128)}) fusion(f32[16,2,4,2,2,128,128]{5,6,3,1,4,2,0:T(8,128)} %convolution_bitcast_fusion.2), kind=kLoop, calls=%fused_computation.17 | loop fusion | flops 4194304 | bytes 50331648 | tf_op jit(solution)/shard_map/sub | solution.py:22
  412.8 9.5 %copy.79 = f32[16,2,4,1,1,128,128]{6,5,2,1,0,4,3:T(8,128)} copy(f32[16,2,4,1,1,128,128]{5,6,3,1,4,2,0:T(8,128)} %get-tuple-element.9) | data formatting | bytes 16777216 | tf_op jit(solution)/shard_map/sub | solution.py:22
  422.3 9.2 %copy.80 = f32[16,2,4,1,1,128,128]{6,5,2,1,0,4,3:T(8,128)} copy(f32[16,2,4,1,1,128,128]{5,6,3,1,4,2,0:T(8,128)} %get-tuple-element.10) | data formatting | bytes 16777216 | tf_op jit(solution)/shard_map/add | solution.py:23
  431.5 6.8 maximum_multiply_fusion.1
  438.3 6.1 copy.85
  444.4 19.3 %slice_subtract_fusion.1 = (f32[16,2,4,1,1,128,128]{5,6,3,1,4,2,0:T(8,128)}, f32[16,2,4,1,1,128,128]{5,6,3,1,4,2,0:T(8,128)}) fusion(f32[16,2,4,2,2,128,128]{5,6,3,1,4,2,0:T(8,128)} %convolution_bitcast_fusion.1), kind=kLoop, calls=%fused_computation.15 | loop fusion | flops 4194304 | bytes 50331648 | tf_op jit(solution)/shard_map/sub | solution.py:22
  463.7 9.2 %copy.91 = f32[16,2,4,1,1,128,128]{6,5,2,1,0,4,3:T(8,128)} copy(f32[16,2,4,1,1,128,128]{5,6,3,1,4,2,0:T(8,128)} %get-tuple-element.7) | data formatting | bytes 16777216 | tf_op jit(solution)/shard_map/sub | solution.py:22
  473.0 9.2 %copy.92 = f32[16,2,4,1,1,128,128]{6,5,2,1,0,4,3:T(8,128)} copy(f32[16,2,4,1,1,128,128]{5,6,3,1,4,2,0:T(8,128)} %get-tuple-element.8) | data formatting | bytes 16777216 | tf_op jit(solution)/shard_map/add | solution.py:23
  482.2 6.8 maximum_multiply_fusion.2
  489.0 6.1 copy.97
  495.1 19.3 %slice_subtract_fusion = (f32[16,2,4,1,1,128,128]{5,6,3,1,4,2,0:T(8,128)}, f32[16,2,4,1,1,128,128]{5,6,3,1,4,2,0:T(8,128)}) fusion(f32[16,2,4,2,2,128,128]{5,6,3,1,4,2,0:T(8,128)} %convolution_bitcast_fusion), kind=kLoop, calls=%fused_computation.13 | loop fusion | flops 4194304 | bytes 50331648 | tf_op jit(solution)/shard_map/sub | solution.py:22
  514.4 9.2 %copy.103 = f32[16,2,4,1,1,128,128]{6,5,2,1,0,4,3:T(8,128)} copy(f32[16,2,4,1,1,128,128]{5,6,3,1,4,2,0:T(8,128)} %get-tuple-element.5) | data formatting | bytes 16777216 | tf_op jit(solution)/shard_map/sub | solution.py:22
  523.6 9.2 %copy.104 = f32[16,2,4,1,1,128,128]{6,5,2,1,0,4,3:T(8,128)} copy(f32[16,2,4,1,1,128,128]{5,6,3,1,4,2,0:T(8,128)} %get-tuple-element.6) | data formatting | bytes 16777216 | tf_op jit(solution)/shard_map/add | solution.py:23
  532.9 6.8 maximum_multiply_fusion.3
  539.7 6.0 copy.109
  545.7 7.9 %broadcast_in_dim.26 = f32[8,16,2,128,128]{4,3,2,1,0:T(8,128)} broadcast(f32[]{:T(128)} %constant.0.clone.1), dimensions={} | broadcast | bytes 16777220 | tf_op jit(solution)/shard_map/broadcast_in_dim | solution.py:52
  553.6 39.5 %scatter_fusion = f32[8,16,2,128,128]{4,3,2,1,0:T(8,128)} fusion(f32[8,16,2,128,128]{4,3,2,1,0:T(8,128)} %broadcast_in_dim.26, s32[128]{0:T(128)S(1)} %copy-done.3, f32[128,2,128,128]{3,2,1,0:T(8,128)} %copy.73), kind=kCustom, calls=%fused_computation | custom fusion | flops 4194304 | bytes 50332672 | tf_op jit(solution)/shard_map/scatter-add | solution.py:30
  593.0 39.8 %scatter_fusion.1 = f32[8,16,2,128,128]{4,3,2,1,0:T(8,128)} fusion(f32[8,16,2,128,128]{4,3,2,1,0:T(8,128)} %scatter_fusion, s32[128]{0:T(128)S(1)} %copy-done.2, f32[128,2,128,128]{3,2,1,0:T(8,128)} %copy.85), kind=kCustom, calls=%fused_computation.1 | custom fusion | flops 4194304 | bytes 50332672 | tf_op jit(solution)/shard_map/scatter-add | solution.py:30
  632.9 39.7 %scatter_fusion.2 = f32[8,16,2,128,128]{4,3,2,1,0:T(8,128)} fusion(f32[8,16,2,128,128]{4,3,2,1,0:T(8,128)} %scatter_fusion.1, s32[128]{0:T(128)S(1)} %copy-done.1, f32[128,2,128,128]{3,2,1,0:T(8,128)} %copy.97), kind=kCustom, calls=%fused_computation.2 | custom fusion | flops 4194304 | bytes 50332672 | tf_op jit(solution)/shard_map/scatter-add | solution.py:30
  672.5 39.7 %scatter_fusion.3 = f32[8,16,2,128,128]{4,3,2,1,0:T(8,128)} fusion(f32[8,16,2,128,128]{4,3,2,1,0:T(8,128)} %scatter_fusion.2, s32[128]{0:T(128)S(1)} %copy-done, f32[128,2,128,128]{3,2,1,0:T(8,128)} %copy.109), kind=kCustom, calls=%fused_computation.3 | custom fusion | flops 4194304 | bytes 50332672 | tf_op jit(solution)/shard_map/scatter-add | solution.py:30
  712.3 9.2 %convert_element_type.55 = bf16[8,16,2,128,128]{4,3,2,1,0:T(8,128)(2,1)} convert(f32[8,16,2,128,128]{4,3,2,1,0:T(8,128)} %scatter_fusion.3) | non-fusion elementwise | flops 4194304 | bytes 25165824 | tf_op jit(solution)/shard_map/convert_element_type | solution.py:77
  (55 shorter events, 6.7 us)
Async XLA Ops:
  6.5 111.2 %all-gather.11.cloned.1.call-start = ((), (), s32[]{:S(2)}) async-start(), calls=%async_computation | async-start | bytes 20971520 | tf_op jit(solution)/shard_map/all_gather | solution.py:54
  7.3 261.4 %all-gather.13.cloned.1.call-start = ((), (), s32[]{:S(2)}) async-start(), calls=%async_computation.1 | async-start | bytes 10485760 | tf_op jit(solution)/shard_map/all_gather | solution.py:63
  473.0 9.2 %copy-start.4 = (f32[128]{0:T(128)S(1)}, f32[128]{0:T(128)}, u32[]{:S(2)}) copy-start(f32[128]{0:T(128)} %reshape.718) | copy-start | bytes 1540
  523.6 9.2 %copy-start.5 = (f32[128]{0:T(128)S(1)}, f32[128]{0:T(128)}, u32[]{:S(2)}) copy-start(f32[128]{0:T(128)} %reshape.719) | copy-start | bytes 1540
  545.7 7.9 %copy-start.3 = (s32[128]{0:T(128)S(1)}, s32[128]{0:T(128)}, u32[]{:S(2)}) copy-start(s32[128]{0:T(128)} %fusion.4) | copy-start | bytes 1540
  553.6 39.5 %copy-start.2 = (s32[128]{0:T(128)S(1)}, s32[128]{0:T(128)}, u32[]{:S(2)}) copy-start(s32[128]{0:T(128)} %fusion.5) | copy-start | bytes 1540
  593.0 39.8 %copy-start.1 = (s32[128]{0:T(128)S(1)}, s32[128]{0:T(128)}, u32[]{:S(2)}) copy-start(s32[128]{0:T(128)} %fusion.6) | copy-start | bytes 1540
  632.9 39.7 %copy-start = (s32[128]{0:T(128)S(1)}, s32[128]{0:T(128)}, u32[]{:S(2)}) copy-start(s32[128]{0:T(128)} %fusion.7) | copy-start | bytes 1540
Sparse Core Ops, SparseCore 0:
  8.9 108.8 all-gather.10
  119.3 149.3 all-gather.12
where the time goes:
time: 733 us; the launch traced here: 729 us
  other arithmetic  275 us (38%)
  waiting for transfers between devices  173 us (24%)
  local copies, waits for them, and re-layouts  139 us (19%)
  matrix products  74 us (10%)
  blocking collectives  51.6 us (7%)
  between operations  15 us (2%)
    scatter-add x4, other arithmetic, pair_products(): total.at[row_index, col_index].add(product.reshape(-1, 2, width, width))  159 us
    all_gather x1, waiting for transfers between devices, body(): lax.all_gather(left_pack[0], 'col', axis=0, tiled=True)  128 us
    sub x4, other arithmetic, pair_products(): real_part = terms[:, :, :, 0, 0] - terms[:, :, :, 1, 1]  77.3 us
    dot_general x4, matrix products, pair_products(): jnp.einsum('kmcij,kndjl->kmncdil', left_blocks, right_blocks, preferred_e...  74 us
    all_gather x1, waiting for transfers between devices, body(): lax.all_gather(right_pack[0], 'row', axis=1, tiled=True)  43.8 us
    sub x4, local copies, waits for them, and re-layouts, pair_products(): real_part = terms[:, :, :, 0, 0] - terms[:, :, :, 1, 1]  37.2 us
    add x4, local copies, waits for them, and re-layouts, pair_products(): imag_part = terms[:, :, :, 0, 1] + terms[:, :, :, 1, 0]  37 us
    mul x4, other arithmetic, pair_products(): jnp.stack([real_part, imag_part], axis=3)  27.1 us
  transfers between devices with their start and end apart: 2, of which 2 were waited for; matrix products, arithmetic and copies ran while one was open for 5% of the time, Pallas kernels for 0%

commit v1 on v0

--- a/solution.py
+++ b/solution.py
@@ -5,6 +5,18 @@
 
 GR = 8
 LEVEL_CUT = 7
+
+
+def doubled_up(shard, axis, dim):
+    ways, here, lap = (lax.axis_size(axis), lax.axis_index(axis), shard.shape[dim])
+    line, have = (shard, 1)
+    while have < ways:
+        line = jnp.concatenate(
+            [line, lax.ppermute(line, axis, [(d, (d - have) % ways) for d in range(ways)])],
+            axis=dim,
+        )
+        have = 2 * have
+    return jnp.roll(line, here * lap, axis=dim)
 
 
 def pair_products(left_pack, right_pack, total):
@@ -60,7 +72,7 @@
     flat = jax.tree.map(lambda member: member.reshape((merged,) + member.shape[2:]), whole)
     carry = total
     piece = (
-        lax.all_gather(left_pack[0], "col", axis=0, tiled=True),
+        doubled_up(left_pack[0], "col", 0),
         lax.all_gather(left_pack[1], "col", axis=0, tiled=True),
         lax.all_gather(left_pack[2], "col", axis=0, tiled=True),
         lax.all_gather(left_pack[3], "col", axis=0, tiled=True),

time: 733 us -> 697 us (0.951)
  blocking collectives: 51.6 us -> 258 us
  waiting for transfers between devices: 173 us -> 0.72 us
  local copies, waits for them, and re-layouts: 139 us -> 38.4 us
  other arithmetic: 275 us -> 299 us
    all_gather x1, blocking collectives: 11.6 us -> 181 us  [body(): lax.all_gather(left_pack[3], 'col', axis=0, tiled=True)]
    all_gather x1 -> x0, waiting for transfers between devices: 128 us -> none  [body(): lax.all_gather(left_pack[0], 'col', axis=0, tiled=True)]
    all_gather x1, waiting for transfers between devices: 43.8 us -> 0.01 us  [body(): lax.all_gather(right_pack[0], 'row', axis=1, tiled=True)]
    all_gather x1, blocking collectives: 10.2 us -> 49.4 us  [body(): lax.all_gather(left_pack[1], 'col', axis=0, tiled=True)]
    sub x4 -> x0, local copies, waits for them, and re-layouts: 37.2 us -> none  [pair_products(): real_part = terms[:, :, :, 0, 0] - terms[:, :, :, 1, 1]]
    add x4 -> x0, local copies, waits for them, and re-layouts: 37 us -> none  [pair_products(): imag_part = terms[:, :, :, 0, 1] + terms[:, :, :, 1, 0]]
    mul x4 -> x0, local copies, waits for them, and re-layouts: 24.3 us -> none  [pair_products(): jnp.stack([real_part, imag_part], axis=3)]
    all_gather x1 -> x0, local copies, waits for them, and re-layouts: 22.7 us -> none  [body(): lax.all_gather(right_pack[0], 'row', axis=1, tiled=True)]
  transfers between devices with their start and end apart: 2 -> 3, of which waited for: 2 -> 0; matrix products, arithmetic and copies ran while one was open for 5% -> 5% of each run, Pallas kernels for 0% -> 0%
where the time goes in v1:
time: 697 us; the launch traced here: 689 us
  other arithmetic  299 us (43%)
  blocking collectives  258 us (37%)
  matrix products  73.6 us (11%)
  local copies, waits for them, and re-layouts  38.4 us (6%)
  between operations  15 us (2%)
    all_gather x1, blocking collectives, body(): lax.all_gather(left_pack[3], 'col', axis=0, tiled=True)  181 us
    scatter-add x4, other arithmetic, pair_products(): total.at[row_index, col_index].add(product.reshape(-1, 2, width, width))  158 us
    sub x4, other arithmetic, pair_products(): real_part = terms[:, :, :, 0, 0] - terms[:, :, :, 1, 1]  77.7 us
    dot_general x4, matrix products, pair_products(): jnp.einsum('kmcij,kndjl->kmncdil', left_blocks, right_blocks, preferred_e...  73.6 us
    all_gather x1, blocking collectives, body(): lax.all_gather(left_pack[1], 'col', axis=0, tiled=True)  49.4 us
    mul x4, other arithmetic, pair_products(): jnp.stack([real_part, imag_part], axis=3)  47.8 us
    unnamed x27, local copies, waits for them, and re-layouts  22.8 us
  transfers between devices with their start and end apart: 3, of which 0 were waited for; matrix products, arithmetic and copies ran while one was open for 5% of the time, Pallas kernels for 0%

profile of v1, /device:TPU:1, one launch (start us, length us, event | category | flops | bytes accessed | tf_op | source)
XLA Modules:
  0.0 689.4 jit_solution(6403553583221109049)
XLA Ops:
  6.5 0.7 all-gather.9.cloned.1.call-update
  7.3 4.2 collective-permute-start
  11.5 0.8 copy.62
  12.2 0.8 copy.59
  13.0 49.4 %all-gather = s32[1,64,2]{2,0,1:T(1,128)S(1)} all-gather(s32[1,16,2]{2,0,1:T(1,128)S(1)} %copy.59), channel_id=2, replica_groups=mesh['kpt'=2,'row'=4,'col'=4] {'col'}, dimensions={1}, use_global_device_ids=true | all-gather | bytes 640 | tf_op jit(solution)/shard_map/all_gather | solution.py:76
  62.4 8.5 %all-gather.1 = s32[1,64,1,4]{3,2,0,1:T(1,128)S(1)} all-gather(s32[1,16,1,4]{3,2,0,1:T(1,128)S(1)} %copy.62), channel_id=3, replica_groups=mesh['kpt'=2,'row'=4,'col'=4] {'row'}, dimensions={1}, use_global_device_ids=true | all-gather | bytes 1280 | tf_op jit(solution)/shard_map/all_gather | solution.py:67
  70.9 4.6 pad_maximum_fusion
  75.5 0.4 collective-permute-start.1
  76.6 1.3 dynamic-slice.1
  77.8 1.3 dynamic-slice
  80.4 0.8 copy.71
  81.1 0.8 copy.68
  81.9 180.7 %all-gather.5 = s32[1,64,2]{2,0,1:T(1,128)S(1)} all-gather(s32[1,16,2]{2,0,1:T(1,128)S(1)} %copy.68), channel_id=7, replica_groups=mesh['kpt'=2,'row'=4,'col'=4] {'col'}, dimensions={1}, use_global_device_ids=true | all-gather | bytes 640 | tf_op jit(solution)/shard_map/all_gather | solution.py:78
  262.6 0.7 bitcast_dynamic-update-slice_fusion
  263.4 6.2 all-reduce.1
  269.5 0.7 bitcast_dynamic-update-slice_fusion.1
  270.3 4.9 all-reduce
  275.1 8.1 %all-gather.6 = s32[1,64,1,4]{3,2,0,1:T(1,128)S(1)} all-gather(s32[1,16,1,4]{3,2,0,1:T(1,128)S(1)} %copy.71), channel_id=8, replica_groups=mesh['kpt'=2,'row'=4,'col'=4] {'row'}, dimensions={1}, use_global_device_ids=true | all-gather | bytes 1280 | tf_op jit(solution)/shard_map/all_gather | solution.py:69
  284.2 0.1 reshape.712
  284.5 0.1 reshape.714
  284.9 0.7 reshape.718
  285.7 0.7 reshape.719
  286.4 0.5 fusion.8
  286.9 0.6 fusion.10
  287.5 3.2 constant_dynamic-update-slice_fusion.5
  290.7 3.2 constant_dynamic-update-slice_fusion.4
  293.9 4.7 constant_dynamic-update-slice_fusion.3
  298.7 1.5 constant_dynamic-update-slice_fusion.2
  300.2 3.2 constant_dynamic-update-slice_fusion.1
  303.3 4.7 constant_dynamic-update-slice_fusion
  308.0 18.4 %convolution_bitcast_fusion.3 = f32[16,2,4,2,2,128,128]{6,5,4,2,3,1,0:T(8,128)} fusion(bf16[1,64,4,2,128,128]{5,4,3,2,1,0:T(8,128)(2,1)} %bitcast.151, bf16[128,2,2,128,128]{4,3,2,1,0:T(8,128)(2,1)} %constant_dynamic-update-slice_fusion, s32[]{:T(128)S(6)} %select_n.96), kind=kOutput, calls=%fused_computation.11 | convolution fusion | flops 2147483648 | bytes 39845892 | tf_op jit(solution)/shard_map/kmcij,kndjl->kmncdil/dot_general | solution.py:31
  326.4 19.8 %slice_subtract_fusion.3 = (f32[16,2,4,1,1,128,128]{6,5,4,2,3,1,0:T(8,128)}, f32[16,2,4,1,1,128,128]{6,5,4,2,3,1,0:T(8,128)}) fusion(f32[16,2,4,2,2,128,128]{6,5,4,2,3,1,0:T(8,128)} %convolution_bitcast_fusion.3), kind=kLoop, calls=%fused_computation.19 | loop fusion | flops 4194304 | bytes 50331648 | tf_op jit(solution)/shard_map/sub | solution.py:34
  346.3 18.4 %convolution_bitcast_fusion.2 = f32[16,2,4,2,2,128,128]{6,5,4,2,3,1,0:T(8,128)} fusion(bf16[1,64,4,2,128,128]{5,4,3,2,1,0:T(8,128)(2,1)} %bitcast.152, bf16[128,2,2,128,128]{4,3,2,1,0:T(8,128)(2,1)} %constant_dynamic-update-slice_fusion, s32[]{:T(128)S(6)} %add.272), kind=kOutput, calls=%fused_computation.10 | convolution fusion | flops 2147483648 | bytes 39845892 | tf_op jit(solution)/shard_map/kmcij,kndjl->kmncdil/dot_general | solution.py:31
  364.7 19.4 %slice_subtract_fusion.2 = (f32[16,2,4,1,1,128,128]{6,5,4,2,3,1,0:T(8,128)}, f32[16,2,4,1,1,128,128]{6,5,4,2,3,1,0:T(8,128)}) fusion(f32[16,2,4,2,2,128,128]{6,5,4,2,3,1,0:T(8,128)} %convolution_bitcast_fusion.2), kind=kLoop, calls=%fused_computation.17 | loop fusion | flops 4194304 | bytes 50331648 | tf_op jit(solution)/shard_map/sub | solution.py:34
  384.0 18.4 %convolution_bitcast_fusion.1 = f32[16,2,4,2,2,128,128]{6,5,4,2,3,1,0:T(8,128)} fusion(bf16[1,64,4,2,128,128]{5,4,3,2,1,0:T(8,128)(2,1)} %bitcast.153, bf16[128,2,2,128,128]{4,3,2,1,0:T(8,128)(2,1)} %constant_dynamic-update-slice_fusion, s32[]{:T(128)S(6)} %add.273), kind=kOutput, calls=%fused_computation.9 | convolution fusion | flops 2147483648 | bytes 39845892 | tf_op jit(solution)/shard_map/kmcij,kndjl->kmncdil/dot_general | solution.py:31
  402.4 19.2 %slice_subtract_fusion.1 = (f32[16,2,4,1,1,128,128]{6,5,4,2,3,1,0:T(8,128)}, f32[16,2,4,1,1,128,128]{6,5,4,2,3,1,0:T(8,128)}) fusion(f32[16,2,4,2,2,128,128]{6,5,4,2,3,1,0:T(8,128)} %convolution_bitcast_fusion.1), kind=kLoop, calls=%fused_computation.15 | loop fusion | flops 4194304 | bytes 50331648 | tf_op jit(solution)/shard_map/sub | solution.py:34
  421.6 18.4 %convolution_bitcast_fusion = f32[16,2,4,2,2,128,128]{6,5,4,2,3,1,0:T(8,128)} fusion(bf16[1,64,4,2,128,128]{5,4,3,2,1,0:T(8,128)(2,1)} %bitcast.154, bf16[128,2,2,128,128]{4,3,2,1,0:T(8,128)(2,1)} %constant_dynamic-update-slice_fusion, s32[]{:T(128)S(6)} %add.274), kind=kOutput, calls=%fused_computation.8 | convolution fusion | flops 2147483648 | bytes 39845892 | tf_op jit(solution)/shard_map/kmcij,kndjl->kmncdil/dot_general | solution.py:31
  440.1 19.3 %slice_subtract_fusion = (f32[16,2,4,1,1,128,128]{6,5,4,2,3,1,0:T(8,128)}, f32[16,2,4,1,1,128,128]{6,5,4,2,3,1,0:T(8,128)}) fusion(f32[16,2,4,2,2,128,128]{6,5,4,2,3,1,0:T(8,128)} %convolution_bitcast_fusion), kind=kLoop, calls=%fused_computation.13 | loop fusion | flops 4194304 | bytes 50331648 | tf_op jit(solution)/shard_map/sub | solution.py:34
  459.4 12.0 %maximum_multiply_fusion = f32[128,2,128,128]{3,2,1,0:T(8,128)} fusion(f32[128,1,128,128]{3,2,1,0:T(8,128)} %bitcast.150, f32[128,1,128,128]{3,2,1,0:T(8,128)} %bitcast.149, f32[128]{0:T(128)S(1)} %reshape.716), kind=kLoop, calls=%fused_computation.4 | loop fusion | flops 8388608 | bytes 33554944 | tf_op jit(solution)/shard_map/mul | solution.py:36
  471.3 7.9 %broadcast_in_dim.26 = f32[8,16,2,128,128]{4,3,2,1,0:T(8,128)} broadcast(f32[]{:T(128)} %constant.27.clone.1), dimensions={} | broadcast | bytes 16777220 | tf_op jit(solution)/shard_map/broadcast_in_dim | solution.py:64
  479.2 39.4 %scatter_fusion = f32[8,16,2,128,128]{4,3,2,1,0:T(8,128)} fusion(f32[8,16,2,128,128]{4,3,2,1,0:T(8,128)} %broadcast_in_dim.26, s32[128]{0:T(128)S(1)} %get-tuple-element.37, f32[128,2,128,128]{3,2,1,0:T(8,128)} %maximum_multiply_fusion), kind=kCustom, calls=%fused_computation | custom fusion | flops 4194304 | bytes 50332672 | tf_op jit(solution)/shard_map/scatter-add | solution.py:42
  518.6 11.9 %maximum_multiply_fusion.1 = f32[128,2,128,128]{3,2,1,0:T(8,128)} fusion(f32[128,1,128,128]{3,2,1,0:T(8,128)} %bitcast.148, f32[128,1,128,128]{3,2,1,0:T(8,128)} %bitcast.147, f32[128]{0:T(128)S(1)} %reshape.717), kind=kLoop, calls=%fused_computation.5 | loop fusion | flops 8388608 | bytes 33554944 | tf_op jit(solution)/shard_map/mul | solution.py:36
  530.6 39.5 %scatter_fusion.1 = f32[8,16,2,128,128]{4,3,2,1,0:T(8,128)} fusion(f32[8,16,2,128,128]{4,3,2,1,0:T(8,128)} %scatter_fusion, s32[128]{0:T(128)S(1)} %copy-done.3, f32[128,2,128,128]{3,2,1,0:T(8,128)} %maximum_multiply_fusion.1), kind=kCustom, calls=%fused_computation.1 | custom fusion | flops 4194304 | bytes 50332672 | tf_op jit(solution)/shard_map/scatter-add | solution.py:42
  570.1 12.0 %maximum_multiply_fusion.2 = f32[128,2,128,128]{3,2,1,0:T(8,128)} fusion(f32[128,1,128,128]{3,2,1,0:T(8,128)} %bitcast.146, f32[128,1,128,128]{3,2,1,0:T(8,128)} %bitcast.145, f32[128]{0:T(128)S(1)} %copy-done.4), kind=kLoop, calls=%fused_computation.6 | loop fusion | flops 8388608 | bytes 33554944 | tf_op jit(solution)/shard_map/mul | solution.py:36
  582.1 39.6 %scatter_fusion.2 = f32[8,16,2,128,128]{4,3,2,1,0:T(8,128)} fusion(f32[8,16,2,128,128]{4,3,2,1,0:T(8,128)} %scatter_fusion.1, s32[128]{0:T(128)S(1)} %copy-done.2, f32[128,2,128,128]{3,2,1,0:T(8,128)} %maximum_multiply_fusion.2), kind=kCustom, calls=%fused_computation.2 | custom fusion | flops 4194304 | bytes 50332672 | tf_op jit(solution)/shard_map/scatter-add | solution.py:42
  621.7 12.0 %maximum_multiply_fusion.3 = f32[128,2,128,128]{3,2,1,0:T(8,128)} fusion(f32[128,1,128,128]{3,2,1,0:T(8,128)} %bitcast.144, f32[128,1,128,128]{3,2,1,0:T(8,128)} %bitcast.143, f32[128]{0:T(128)S(1)} %copy-done.5), kind=kLoop, calls=%fused_computation.7 | loop fusion | flops 8388608 | bytes 33554944 | tf_op jit(solution)/shard_map/mul | solution.py:36
  633.6 39.6 %scatter_fusion.3 = f32[8,16,2,128,128]{4,3,2,1,0:T(8,128)} fusion(f32[8,16,2,128,128]{4,3,2,1,0:T(8,128)} %scatter_fusion.2, s32[128]{0:T(128)S(1)} %copy-done.1, f32[128,2,128,128]{3,2,1,0:T(8,128)} %maximum_multiply_fusion.3), kind=kCustom, calls=%fused_computation.3 | custom fusion | flops 4194304 | bytes 50332672 | tf_op jit(solution)/shard_map/scatter-add | solution.py:42
  673.2 9.2 %convert_element_type.55 = bf16[8,16,2,128,128]{4,3,2,1,0:T(8,128)(2,1)} convert(f32[8,16,2,128,128]{4,3,2,1,0:T(8,128)} %scatter_fusion.3) | non-fusion elementwise | flops 4194304 | bytes 25165824 | tf_op jit(solution)/shard_map/convert_element_type | solution.py:89
  (48 shorter events, 2.1 us)
Async XLA Ops:
  6.5 292.1 %copy-start = (bf16[1,16,2,2,128,128]{5,4,3,2,1,0:T(8,128)(2,1)S(1)}, bf16[1,16,2,2,128,128]{5,4,3,2,1,0:T(8,128)(2,1)}, u32[]{:S(2)}) copy-start(bf16[1,16,2,2,128,128]{5,4,3,2,1,0:T(8,128)(2,1)} %param.8) | copy-start | bytes 6291460
  6.5 301.5 %all-gather.9.cloned.1.call-start = ((), (), s32[]{:S(2)}) async-start(), calls=%async_computation | async-start | bytes 20971520 | tf_op jit(solution)/shard_map/all_gather | solution.py:66
  7.3 63.7 %collective-permute-start = (bf16[16,2,2,128,128]{4,3,2,1,0:T(8,128)(2,1)}, bf16[16,2,2,128,128]{4,3,2,1,0:T(8,128)(2,1)}, u32[]{:S(2)}, u32[]{:S(2)}) collective-permute-start(bf16[16,2,2,128,128]{4,3,2,1,0:T(8,128)(2,1)} %bitcast.155), channel_id=1, source_target_pairs={{0,3},{1,0},{2,1},{3,2},{4,7},{5,4},{6,5},{7,6},{8,11},{9,8},{10,9... | collective-permute-start | bytes 6291464 | tf_op jit(solution)/shard_map/ppermute | solution.py:15
  75.5 218.4 %collective-permute-start.1 = (bf16[32,2,2,128,128]{4,3,2,1,0:T(8,128)(2,1)}, bf16[32,2,2,128,128]{4,3,2,1,0:T(8,128)(2,1)}, u32[]{:S(2)}, u32[]{:S(2)}) collective-permute-start(bf16[32,2,2,128,128]{4,3,2,1,0:T(8,128)(2,1)} %pad_maximum_fusion), channel_id=1, source_target_pairs={{0,2},{1,3},{2,0},{3,1},{4,6},{5,7},{6,4},{7,5},{8,10},{9,11},{10,... | collective-permute-start | bytes 12582920 | tf_op jit(solution)/shard_map/ppermute | solution.py:15
  518.6 12.0 %copy-start.3 = (s32[128]{0:T(128)S(1)}, s32[128]{0:T(128)}, u32[]{:S(2)}) copy-start(s32[128]{0:T(128)} %get-tuple-element.38) | copy-start | bytes 1540
  530.6 39.5 %copy-start.4 = (f32[128]{0:T(128)S(1)}, f32[128]{0:T(128)}, u32[]{:S(2)}) copy-start(f32[128]{0:T(128)} %reshape.718) | copy-start | bytes 1540
  570.1 12.0 %copy-start.2 = (s32[128]{0:T(128)S(1)}, s32[128]{0:T(128)}, u32[]{:S(2)}) copy-start(s32[128]{0:T(128)} %get-tuple-element.39) | copy-start | bytes 1540
  582.1 39.6 %copy-start.5 = (f32[128]{0:T(128)S(1)}, f32[128]{0:T(128)}, u32[]{:S(2)}) copy-start(f32[128]{0:T(128)} %reshape.719) | copy-start | bytes 1540
  621.7 12.0 %copy-start.1 = (s32[128]{0:T(128)S(1)}, s32[128]{0:T(128)}, u32[]{:S(2)}) copy-start(s32[128]{0:T(128)} %get-tuple-element.40) | copy-start | bytes 1540
Sparse Core Ops, SparseCore 0:
  8.9 108.5 all-gather.8
